TPU v7x, 32 devices: a whole 2x2x4 slice. The times are simulated.
32 devices in a mesh: groups: 2 (over y), seq: 4 (over z), role: 2 (over x), mb: 2 (over core).
Axes of the slice: x: 2, y: 2, z: 4, core: 2. Of those that a mesh axis runs over, the one named last changes fastest.
Arguments:
- queries: bfloat16 [256, 128, 576], P(('groups', 'seq'), ('role', 'mb')), parts along dimension 0, may hold values from -200 to 200
- cache: bfloat16 [256, 256, 576], P(('groups', 'seq')), parts along dimension 0, may hold values from -24 to 24
- lengths: int32 [256], P(('groups', 'seq')), parts along dimension 0, may hold values from 2 to 256
- w_uv: bfloat16 [128, 512, 128], P(('role', 'mb'), None, 'seq'), may hold values from -0.25 to 0.25
- w_o: bfloat16 [128, 128, 3584], P(('role', 'mb'), 'seq'), may hold values from -0.1875 to 0.1875
- x_in: bfloat16 [256, 3584], P('groups', 'seq'), parts along dimension 0, may hold values from -16 to 16
- norm_gain: float32 [3584], P('seq'), may hold values from 0.1 to 1.9
- w_gate: bfloat16 [8, 3584, 2048], P(('seq', 'mb'), None, 'role'), may hold values from -0.09375 to 0.09375
- w_up: bfloat16 [8, 3584, 2048], P(('seq', 'mb'), None, 'role'), may hold values from -0.09375 to 0.09375
- w_down: bfloat16 [8, 2048, 3584], P(('seq', 'mb'), 'role'), may hold values from -0.125 to 0.125
- expert_ids: int32 [256, 2], P('groups'), parts along dimension 0, may hold values from 0 to 7, all different within a row; in each aligned block of 128 rows (0 to 127, 128 to 255, ...) at most 64 rows name the same one
- gate_weights: float32 [256, 2], P('groups'), parts along dimension 0, may hold values from 0.2 to 1
- expert_slot: int32 [8], replicated, may hold values from 0 to 7, each once
Outputs:
- layer_out: bfloat16 [256, 3584], P('groups', 'seq'), parts along dimension 0
There are 2 independent parts, one for each index of `groups`. A program takes and returns all parts, laid end to end along the dimension named above; an argument that names none is the same for every part. Nothing has to cross between parts.
Inputs may be any that keep to these rules, and one draw needn't show every extreme that they name: `expert_ids`: each row names 2 different experts; over the rows of one group no expert is named more than 64 times, a bound that some block reaches. A permutation: expert e uses the weights at index expert_slot[e].
All inputs are finite; a program needn't handle non-finite values.
Results may differ from a plain program's by a relative error of at most 0.012.
Values may be sent and summed in bfloat16 or wider, within the bound.
No kernel may reach another device: no remote copies, remote signals or barrier semaphores. Data moves between devices by JAX's collectives and lax.ppermute only.
A program may use at most 128 MiB of HBM per device.

v0:
```python
import jax
import jax.numpy as jnp
from jax import lax
from jax.sharding import PartitionSpec as P

D = 3584
LAT = 512
ROPE = 64
VH = 128
ROWS = 128
CAP = 64


def per_device(
    queries,
    cache,
    lengths,
    w_uv,
    w_o,
    x_in,
    norm_gain,
    w_gate,
    w_up,
    w_down,
    expert_ids,
    gate_weights,
    expert_slot,
):
    score_scale = (VH + ROPE) ** (-0.5)
    cache_span = cache.shape[1]
    positions = jnp.arange(cache_span, dtype=jnp.int32)
    valid_mask = positions[None, :] < lengths[:, None]
    scores = (
        jnp.einsum("bhd,btd->bht", queries, cache, preferred_element_type=jnp.float32) * score_scale
    )
    scores = jnp.where(valid_mask[:, None, :], scores, -1e30)
    row_max = jnp.max(scores, axis=2)
    exp_scores = jnp.where(valid_mask[:, None, :], jnp.exp(scores - row_max[:, :, None]), 0.0)
    denominator = jnp.sum(exp_scores, axis=2)
    numerator = jnp.einsum(
        "bht,btc->bhc",
        exp_scores.astype(jnp.bfloat16),
        cache[:, :, :LAT],
        preferred_element_type=jnp.float32,
    )
    latent = (numerator / denominator[:, :, None]).astype(jnp.bfloat16)
    latent = lax.all_gather(latent, "seq", axis=0, tiled=True)
    values = jnp.einsum("bhc,hcj->bhj", latent, w_uv, preferred_element_type=jnp.float32).astype(
        jnp.bfloat16
    )
    attn_term = jnp.einsum("bhj,hjd->bd", values, w_o, preferred_element_type=jnp.float32)
    col_part = lax.psum_scatter(attn_term, "seq", scatter_dimension=1, tiled=True)
    attention = lax.psum(col_part, ("role", "mb"))
    hidden = x_in.astype(jnp.float32) + attention
    squares = lax.psum(jnp.sum(hidden * hidden, axis=1), "seq")
    normed = (hidden * lax.rsqrt(squares[:, None] / D + 1e-06) * norm_gain[None, :]).astype(
        jnp.bfloat16
    )
    seq_count = lax.axis_size("seq")
    pair_count = lax.axis_size("mb")
    pair_index = lax.axis_index("mb")
    expert_count = expert_slot.shape[0]
    expert_range = jnp.arange(expert_count, dtype=jnp.int32)
    named_mask = expert_ids[:, :, None] == expert_range[None, None, :]
    slot_of = jnp.sum(jnp.where(named_mask, expert_slot[None, None, :], 0), axis=2)
    chosen = slot_of[:, :, None] == expert_range[None, None, :]
    member = jnp.any(chosen, axis=1).astype(jnp.int32)
    gate_slot = jnp.sum(jnp.where(chosen, gate_weights[:, :, None], 0.0), axis=1)
    position = jnp.cumsum(member, axis=0) - member
    slot_range = jnp.arange(CAP, dtype=jnp.int32)
    select = (member.T[:, None, :] == 1) & (position.T[:, None, :] == slot_range[None, :, None])
    select_own = lax.dynamic_index_in_dim(
        select.reshape(seq_count, pair_count, CAP, ROWS), pair_index, 1, keepdims=False
    )
    gate_own = lax.dynamic_index_in_dim(
        gate_slot.T.reshape(seq_count, pair_count, ROWS), pair_index, 1, keepdims=False
    )
    select_half = select_own.astype(jnp.bfloat16)
    gathered = lax.all_gather(normed, "seq", axis=1, tiled=True)
    mine = lax.dynamic_index_in_dim(select_half, lax.axis_index("seq"), 0, keepdims=False)
    picked = jnp.dot(mine, gathered, preferred_element_type=jnp.float32).astype(jnp.bfloat16)
    incoming = picked[None]
    item_count = incoming.shape[1]
    rows_in = incoming.reshape(item_count, incoming.shape[2])
    gate_out = jnp.dot(rows_in, w_gate[0], preferred_element_type=jnp.float32)
    up_out = jnp.dot(rows_in, w_up[0], preferred_element_type=jnp.float32)
    activated = (jax.nn.silu(gate_out) * up_out).astype(jnp.bfloat16)
    result = jnp.dot(activated, w_down[0], preferred_element_type=jnp.float32)
    returned = lax.all_to_all(
        result[None].astype(jnp.bfloat16), "seq", split_axis=2, concat_axis=0, tiled=True
    ).astype(jnp.float32)
    mixing = select_own.astype(jnp.float32) * gate_own[:, None, :]
    partial_mix = jnp.einsum("tcb,tcd->bd", mixing, returned, precision=lax.Precision.HIGHEST)
    expert_mix = lax.psum(partial_mix.astype(jnp.bfloat16), ("role", "mb")).astype(jnp.float32)
    return (hidden + expert_mix).astype(jnp.bfloat16)


def solution(mesh):
    in_specs = (
        P(("groups", "seq"), ("role", "mb"), None),
        P(("groups", "seq"), None, None),
        P(("groups", "seq")),
        P(("role", "mb"), None, "seq"),
        P(("role", "mb"), "seq", None),
        P("groups", "seq"),
        P("seq"),
        P(("seq", "mb"), None, "role"),
        P(("seq", "mb"), None, "role"),
        P(("seq", "mb"), "role", None),
        P("groups", None),
        P("groups", None),
        P(),
    )
    out_specs = P("groups", "seq")
    return jax.shard_map(
        per_device, mesh=mesh, in_specs=in_specs, out_specs=out_specs, check_vma=False
    )
```

profile of v0, /device:TPU:0, one launch (start us, length us, event | category | flops | bytes accessed | tf_op | source)
XLA Modules:
  0.0 318.2 jit_solution(6320305931758377276)
XLA Ops:
  6.5 0.0 copy-start
  6.5 0.0 all-gather.2.cloned.1.call-start
  6.5 0.8 iota_compare_fusion.1
  7.4 0.5 copy-done
  7.9 5.5 %fusion.61 = (f32[32,32]{1,0:T(8,128)S(1)}, bf16[32,32,256]{2,1,0:T(8,128)(2,1)S(1)}) fusion(pred[32,256]{1,0:T(8,128)(4,1)S(1)} %iota_compare_fusion.1, bf16[32,32,576]{2,1,0:T(8,128)(2,1)S(1)} %copy-done, bf16[32,256,576]{1,2,0:T(8,128)(2,1)} %param.14), kind=kOutput, calls=%fused_computation.62 | convolution fusion | flops 303563008 | bytes 11153408 | tf_op jit(solution)/shard_map/sub | solution.py:38
  13.3 7.0 %divide_convert_fusion = bf16[32,32,512]{2,1,0:T(8,128)(2,1)} fusion(f32[32,32]{1,0:T(8,128)S(1)} %get-tuple-element.7, bf16[32,256,576]{1,2,0:T(8,128)(2,1)} %param.14, bf16[32,32,256]{2,1,0:T(8,128)(2,1)S(1)} %get-tuple-element.8), kind=kOutput, calls=%fused_computation.15 | convolution fusion | flops 269484032 | bytes 9965568 | tf_op jit(solution)/shard_map/bht,btc->bhc/dot_general | solution.py:40
  20.3 0.0 all-gather.2.cloned.1.call-update
  20.4 0.0 copy-start.4
  20.4 0.0 copy-start.6
  20.4 0.0 copy-start.1
  20.4 0.0 copy-start.3
  20.4 0.0 reduce-scatter.2.cloned.1.call-start
  20.5 83.5 %all-gather.2.cloned.1.call-done = bf16[128,32,512]{2,1,0:T(8,128)(2,1)} async-done(((bf16[32,32,512]{2,1,0:T(8,128)(2,1)}), bf16[128,32,512]{2,1,0:T(8,128)(2,1)}) %all-gather.2.cloned.1.call-update) | async-done | bytes 4194320 | tf_op jit(solution)/shard_map/all_gather | solution.py:47
  104.0 0.0 copy-done.2
  104.0 9.0 %convolution_bitcast_fusion = f32[128,3584]{1,0:T(8,128)} fusion(bf16[32,32,3584]{2,1,0:T(8,128)(2,1)} %param.17, bf16[32,512,32]{1,2,0:T(8,128)(2,1)S(1)} %copy-done.2, bf16[128,32,512]{2,1,0:T(8,128)(2,1)} %all-gather.2.cloned.1.call-done), kind=kOutput, calls=%fused_computation.9 | convolution fusion | flops 1073872896 | bytes 14417920 | tf_op jit(solution)/shard_map/bhj,hjd->bd/dot_general | solution.py:51
  113.0 0.0 reduce-scatter.2.cloned.1.call-update
  113.0 0.0 all-reduce.3.cloned.1.call-start
  113.1 0.0 copy-done.4
  113.1 0.0 copy-done.6
  113.1 0.1 select_reduce_fusion.1
  113.2 0.1 copy.48
  113.3 0.2 reduce_window_sum.11
  113.5 37.7 %reduce-scatter.2.cloned.1.call-done = f32[128,896]{1,0:T(8,128)} async-done(((f32[128,3584]{1,0:T(8,128)}), f32[128,896]{1,0:T(8,128)}) %reduce-scatter.2.cloned.1.call-update) | async-done | bytes 458768 | tf_op jit(solution)/shard_map/reduce_scatter | solution.py:52
  151.2 0.0 all-reduce.3.cloned.1.call-update
  151.3 0.1 copy.49
  151.4 0.1 fusion.47
  151.5 34.2 %all-reduce.3.cloned.1.call-done = f32[128,896]{1,0:T(8,128)} async-done(((f32[128,896]{1,0:T(8,128)}), f32[128,896]{1,0:T(8,128)}) %all-reduce.3.cloned.1.call-update) | async-done | bytes 458768 | tf_op jit(solution)/shard_map/psum | solution.py:53
  185.7 1.2 multiply_reduce_fusion
  186.9 11.8 %psum.22 = f32[128]{0:T(128)S(1)} all-reduce(f32[128]{0:T(128)S(1)} %multiply_reduce_fusion), channel_id=1, replica_groups=mesh['groups'=2,'seq'=4,'role'=2,'mb'=2] {'seq'}, use_global_device_ids=true, to_apply=%region_9.10 | all-reduce | flops 128 | bytes 1024 | tf_op jit(solution)/shard_map/psum | solution.py:55
  198.7 1.1 multiply_convert_fusion
  199.8 18.0 %all_gather.7 = bf16[128,3584]{1,0:T(8,128)(2,1)S(1)} all-gather(bf16[128,896]{1,0:T(8,128)(2,1)S(1)} %multiply_convert_fusion), channel_id=1, replica_groups=mesh['groups'=2,'seq'=4,'role'=2,'mb'=2] {'seq'}, dimensions={1}, use_global_device_ids=true | all-gather | bytes 1146880 | tf_op jit(solution)/shard_map/all_gather | solution.py:79
  217.8 0.3 convolution_convert_fusion
  218.1 4.5 %fusion.7 = f32[64,1024]{1,0:T(8,128)S(1)} fusion(bf16[64,3584]{1,0:T(8,128)(2,1)S(1)} %convolution_convert_fusion, bf16[1,3584,1024]{2,1,0:T(8,128)(2,1)} %param.20), kind=kOutput, calls=%fused_computation.7 | convolution fusion | flops 469762048 | bytes 8060928 | tf_op jit(solution)/shard_map/dot_general | solution.py:85
  222.6 8.6 %fusion.12 = bf16[1,64,3584]{2,1,0:T(8,128)(2,1)} fusion(bf16[1,1024,3584]{2,1,0:T(8,128)(2,1)} %param.22, bf16[64,3584]{1,0:T(8,128)(2,1)S(1)} %convolution_convert_fusion, bf16[1,3584,1024]{2,1,0:T(8,128)(2,1)} %param.21, f32[64,1024]{1,0:T(8,128)S(1)} %fusion.7), kind=kOutput, calls=%fused_computation.12 | convolution fusion | flops 940146688 | bytes 15859712 | tf_op jit(solution)/shard_map/dot_general | solution.py:88
  231.2 4.2 %copy.53 = bf16[1,64,3584]{1,0,2:T(2,128)(2,1)S(1)} copy(bf16[1,64,3584]{2,1,0:T(8,128)(2,1)} %fusion.12) | data formatting | bytes 917504 | tf_op jit(solution)/shard_map/convert_element_type | solution.py:90
  235.4 0.5 broadcast.36
  236.0 20.6 %reduce = bf16[3584,64]{1,0:T(8,128)(2,1)} reduce(bf16[3584,1,64]{2,1,0:T(2,128)(2,1)S(1)} %bitcast.64, bf16[]{:T(256)} %broadcast.36), dimensions={1}, to_apply=%bitcast.54.reduce_sub_computation | reduce | bytes 917506
  256.6 2.8 reshape.46
  259.4 4.1 %all-to-all-start = ((bf16[4,2,28672]{2,1,0:T(2,128)(2,1)}), bf16[4,2,28672]{2,1,0:T(2,128)(2,1)}, u32[]{:S(2)}, u32[]{:S(2)}) async-start(bf16[4,2,28672]{2,1,0:T(2,128)(2,1)} %reshape.46), calls=%async_computation.1 | async-start | bytes 917504 | tf_op jit(solution)/shard_map/all_to_all | solution.py:89
  263.6 0.0 all-reduce.5.cloned.1.call-start
  263.6 9.6 %all-to-all-done = bf16[4,2,28672]{2,1,0:T(2,128)(2,1)} async-done(((bf16[4,2,28672]{2,1,0:T(2,128)(2,1)}), bf16[4,2,28672]{2,1,0:T(2,128)(2,1)}, u32[]{:S(2)}, u32[]{:S(2)}) %all-to-all-start) | async-done | bytes 458784 | tf_op jit(solution)/shard_map/all_to_all | solution.py:89
  273.2 2.4 reshape.47
  275.6 1.0 copy.58
  276.7 1.5 copy.55
  278.2 1.1 fusion.24
  279.3 0.0 all-reduce.5.cloned.1.call-update
  279.3 30.5 %all-reduce.5.cloned.1.call-done = bf16[128,896]{1,0:T(8,128)(2,1)} async-done(((bf16[128,896]{1,0:T(8,128)(2,1)}), bf16[128,896]{1,0:T(8,128)(2,1)}) %all-reduce.5.cloned.1.call-update) | async-done | bytes 229392 | tf_op jit(solution)/shard_map/psum | solution.py:94
  309.8 1.9 add_convert_fusion
  (15 shorter events, 0.2 us)
Async XLA Ops:
  6.5 1.3 copy-start
  6.5 97.4 %all-gather.2.cloned.1.call-start = ((), (), s32[]{:S(2)}) async-start(), calls=%async_computation.2 | async-start | bytes 5242880 | tf_op jit(solution)/shard_map/all_gather | solution.py:47
  13.3 90.6 %copy-start.2 = (bf16[32,512,32]{1,2,0:T(8,128)(2,1)S(1)}, bf16[32,512,32]{1,2,0:T(8,128)(2,1)}, u32[]{:S(2)}) copy-start(bf16[32,512,32]{1,2,0:T(8,128)(2,1)} %param.16) | copy-start | bytes 3145732
  20.4 92.7 %copy-start.4 = (s32[128,2]{0,1:T(2,128)S(1)}, s32[128,2]{0,1:T(2,128)}, u32[]{:S(2)}) copy-start(s32[128,2]{0,1:T(2,128)} %param.23) | copy-start | bytes 3076
  20.4 92.7 %copy-start.6 = (s32[8]{0:T(128)S(1)}, s32[8]{0:T(128)}, u32[]{:S(2)}) copy-start(s32[8]{0:T(128)} %param.25) | copy-start | bytes 100
  20.4 165.3 %copy-start.1 = (bf16[128,896]{1,0:T(8,128)(2,1)S(1)}, bf16[128,896]{1,0:T(8,128)(2,1)}, u32[]{:S(2)}) copy-start(bf16[128,896]{1,0:T(8,128)(2,1)} %param.18) | copy-start | bytes 688132
  20.4 178.3 %copy-start.3 = (f32[896]{0:T(1024)S(1)}, f32[896]{0:T(1024)}, u32[]{:S(2)}) copy-start(f32[896]{0:T(1024)} %param.19) | copy-start | bytes 10756
  20.4 130.8 %reduce-scatter.2.cloned.1.call-start = ((), (), s32[]{:S(2)}) async-start(), calls=%async_computation.3 | async-start | bytes 2293760 | tf_op jit(solution)/shard_map/reduce_scatter | solution.py:52
  113.0 72.7 %all-reduce.3.cloned.1.call-start = ((), (), s32[]{:S(2)}) async-start(), calls=%async_computation.4 | async-start | bytes 917504 | tf_op jit(solution)/shard_map/psum | solution.py:53
  231.2 32.4 %copy-start.5 = (f32[128,2]{0,1:T(2,128)S(1)}, f32[128,2]{0,1:T(2,128)}, u32[]{:S(2)}) copy-start(f32[128,2]{0,1:T(2,128)} %param.24) | copy-start | bytes 3076
  259.4 13.8 %all-to-all-start = ((bf16[4,2,28672]{2,1,0:T(2,128)(2,1)}), bf16[4,2,28672]{2,1,0:T(2,128)(2,1)}, u32[]{:S(2)}, u32[]{:S(2)}) async-start(bf16[4,2,28672]{2,1,0:T(2,128)(2,1)} %reshape.46), calls=%async_computation.1 | async-start | bytes 917504 | tf_op jit(solution)/shard_map/all_to_all | solution.py:89
  263.6 46.3 %all-reduce.5.cloned.1.call-start = ((), (), s32[]{:S(2)}) async-start(), calls=%async_computation.5 | async-start | bytes 458752 | tf_op jit(solution)/shard_map/psum | solution.py:94
Sparse Core Ops, SparseCore 0:
  20.5 83.4 all-gather.1
  113.1 37.9 reduce-scatter.1
  153.5 32.1 all-reduce.2
  279.5 30.3 all-reduce.4
where the time goes:
time: 319 us; the launch traced here: 318 us
  waiting for transfers between devices  196 us (61%)
  matrix products  36 us (11%)
  blocking collectives  29.8 us (9%)
  other arithmetic  26 us (8%)
  local copies, waits for them, and re-layouts  13.4 us (4%)
  between operations  13.3 us (4%)
  starting transfers between devices  4.25 us (1%)
    all_gather x1, waiting for transfers between devices, per_device(): latent = lax.all_gather(latent, 'seq', axis=0, tiled=True)  83.5 us
    reduce_scatter x1, waiting for transfers between devices, per_device(): lax.psum_scatter(attn_term, 'seq', scatter_dimension=1, tiled=True)  37.7 us
    psum x1, waiting for transfers between devices, per_device(): attention = lax.psum(col_part, ('role', 'mb'))  34.2 us
    psum x1, waiting for transfers between devices, per_device(): lax.psum(partial_mix.astype(jnp.bfloat16), ('role', 'mb'))  30.5 us
    unnamed x1, other arithmetic  20.6 us
    all_gather x1, blocking collectives, per_device(): gathered = lax.all_gather(normed, 'seq', axis=1, tiled=True)  18 us
    psum x1, blocking collectives, per_device(): squares = lax.psum(jnp.sum(hidden * hidden, axis=1), 'seq')  11.8 us
    all_to_all x1, waiting for transfers between devices, per_device(): lax.all_to_all(result[None].astype(jnp.bfloat16), 'seq', split_axis=2, co...  9.55 us
  transfers between devices with their start and end apart: 5, of which 5 were waited for; matrix products, arithmetic and copies ran while one was open for 0% of the time, Pallas kernels for 0%

commit v1 on v0

--- a/solution.py
+++ b/solution.py
@@ -91,7 +91,9 @@
     ).astype(jnp.float32)
     mixing = select_own.astype(jnp.float32) * gate_own[:, None, :]
     partial_mix = jnp.einsum("tcb,tcd->bd", mixing, returned, precision=lax.Precision.HIGHEST)
-    expert_mix = lax.psum(partial_mix.astype(jnp.bfloat16), ("role", "mb")).astype(jnp.float32)
+    expert_mix = lax.psum(lax.psum(partial_mix.astype(jnp.bfloat16), "mb"), "role").astype(
+        jnp.float32
+    )
     return (hidden + expert_mix).astype(jnp.bfloat16)
 
 

time: 319 us -> 331 us (1.038)
  waiting for transfers between devices: 196 us -> 208 us
    psum x1 -> x2, waiting for transfers between devices: 30.5 us -> 42.6 us  [the longest x1 26.2 us: per_device(): lax.psum(lax.psum(partial_mix.astype(jnp.bfloat16), 'mb'), 'role')]
  transfers between devices with their start and end apart: 5 -> 6, of which waited for: 5 -> 6; matrix products, arithmetic and copies ran while one was open for 0% -> 0% of each run, Pallas kernels for 0% -> 0%
where the time goes in v1:
time: 331 us; the launch traced here: 330 us
  waiting for transfers between devices  208 us (63%)
  matrix products  36 us (11%)
  blocking collectives  29.8 us (9%)
  other arithmetic  26 us (8%)
  local copies, waits for them, and re-layouts  13.4 us (4%)
  between operations  13.3 us (4%)
  starting transfers between devices  4.29 us (1%)
    all_gather x1, waiting for transfers between devices, per_device(): latent = lax.all_gather(latent, 'seq', axis=0, tiled=True)  83.5 us
    reduce_scatter x1, waiting for transfers between devices, per_device(): lax.psum_scatter(attn_term, 'seq', scatter_dimension=1, tiled=True)  37.7 us
    psum x1, waiting for transfers between devices, per_device(): attention = lax.psum(col_part, ('role', 'mb'))  34.2 us
    psum x1, waiting for transfers between devices, per_device(): lax.psum(lax.psum(partial_mix.astype(jnp.bfloat16), 'mb'), 'role')  26.2 us
    unnamed x1, other arithmetic  20.6 us
    all_gather x1, blocking collectives, per_device(): gathered = lax.all_gather(normed, 'seq', axis=1, tiled=True)  18 us
    psum x1, waiting for transfers between devices, per_device(): lax.psum(partial_mix.astype(jnp.bfloat16), 'mb')  16.4 us
    psum x1, blocking collectives, per_device(): squares = lax.psum(jnp.sum(hidden * hidden, axis=1), 'seq')  11.8 us
  transfers between devices with their start and end apart: 6, of which 6 were waited for; matrix products, arithmetic and copies ran while one was open for 0% of the time, Pallas kernels for 0%

profile of v1, /device:TPU:0, one launch (start us, length us, event | category | flops | bytes accessed | tf_op | source)
XLA Modules:
  0.0 330.4 jit_solution(12935544190334530825)
XLA Ops:
  6.5 0.0 all-gather.2.cloned.1.call-start
  6.5 0.8 iota_compare_fusion.1
  7.4 0.5 copy-done
  7.9 5.5 %fusion.61 = (f32[32,32]{1,0:T(8,128)S(1)}, bf16[32,32,256]{2,1,0:T(8,128)(2,1)S(1)}) fusion(pred[32,256]{1,0:T(8,128)(4,1)S(1)} %iota_compare_fusion.1, bf16[32,32,576]{2,1,0:T(8,128)(2,1)S(1)} %copy-done, bf16[32,256,576]{1,2,0:T(8,128)(2,1)} %param.14), kind=kOutput, calls=%fused_computation.62 | convolution fusion | flops 303563008 | bytes 11153408 | tf_op jit(solution)/shard_map/sub | solution.py:38
  13.3 7.0 %divide_convert_fusion = bf16[32,32,512]{2,1,0:T(8,128)(2,1)} fusion(f32[32,32]{1,0:T(8,128)S(1)} %get-tuple-element.7, bf16[32,256,576]{1,2,0:T(8,128)(2,1)} %param.14, bf16[32,32,256]{2,1,0:T(8,128)(2,1)S(1)} %get-tuple-element.8), kind=kOutput, calls=%fused_computation.15 | convolution fusion | flops 269484032 | bytes 9965568 | tf_op jit(solution)/shard_map/bht,btc->bhc/dot_general | solution.py:40
  20.3 0.0 all-gather.2.cloned.1.call-update
  20.4 0.0 copy-start.4
  20.4 0.0 copy-start.6
  20.4 0.0 copy-start.1
  20.4 0.0 copy-start.3
  20.4 0.0 reduce-scatter.2.cloned.1.call-start
  20.5 83.5 %all-gather.2.cloned.1.call-done = bf16[128,32,512]{2,1,0:T(8,128)(2,1)} async-done(((bf16[32,32,512]{2,1,0:T(8,128)(2,1)}), bf16[128,32,512]{2,1,0:T(8,128)(2,1)}) %all-gather.2.cloned.1.call-update) | async-done | bytes 4194320 | tf_op jit(solution)/shard_map/all_gather | solution.py:47
  104.0 0.0 copy-done.2
  104.0 9.0 %convolution_bitcast_fusion = f32[128,3584]{1,0:T(8,128)} fusion(bf16[32,32,3584]{2,1,0:T(8,128)(2,1)} %param.17, bf16[32,512,32]{1,2,0:T(8,128)(2,1)S(1)} %copy-done.2, bf16[128,32,512]{2,1,0:T(8,128)(2,1)} %all-gather.2.cloned.1.call-done), kind=kOutput, calls=%fused_computation.9 | convolution fusion | flops 1073872896 | bytes 14417920 | tf_op jit(solution)/shard_map/bhj,hjd->bd/dot_general | solution.py:51
  113.0 0.0 reduce-scatter.2.cloned.1.call-update
  113.0 0.0 all-reduce.4.cloned.1.call-start
  113.1 0.1 select_reduce_fusion.1
  113.2 0.1 copy.48
  113.3 0.2 reduce_window_sum.11
  113.5 37.7 %reduce-scatter.2.cloned.1.call-done = f32[128,896]{1,0:T(8,128)} async-done(((f32[128,3584]{1,0:T(8,128)}), f32[128,896]{1,0:T(8,128)}) %reduce-scatter.2.cloned.1.call-update) | async-done | bytes 458768 | tf_op jit(solution)/shard_map/reduce_scatter | solution.py:52
  151.2 0.0 all-reduce.4.cloned.1.call-update
  151.3 0.1 copy.49
  151.4 0.1 fusion.47
  151.5 34.2 %all-reduce.4.cloned.1.call-done = f32[128,896]{1,0:T(8,128)} async-done(((f32[128,896]{1,0:T(8,128)}), f32[128,896]{1,0:T(8,128)}) %all-reduce.4.cloned.1.call-update) | async-done | bytes 458768 | tf_op jit(solution)/shard_map/psum | solution.py:53
  185.7 1.2 multiply_reduce_fusion
  186.9 11.8 %psum.29 = f32[128]{0:T(128)S(1)} all-reduce(f32[128]{0:T(128)S(1)} %multiply_reduce_fusion), channel_id=1, replica_groups=mesh['groups'=2,'seq'=4,'role'=2,'mb'=2] {'seq'}, use_global_device_ids=true, to_apply=%region_9.10 | all-reduce | flops 128 | bytes 1024 | tf_op jit(solution)/shard_map/psum | solution.py:55
  198.7 1.1 multiply_convert_fusion
  199.8 18.0 %all_gather.7 = bf16[128,3584]{1,0:T(8,128)(2,1)S(1)} all-gather(bf16[128,896]{1,0:T(8,128)(2,1)S(1)} %multiply_convert_fusion), channel_id=1, replica_groups=mesh['groups'=2,'seq'=4,'role'=2,'mb'=2] {'seq'}, dimensions={1}, use_global_device_ids=true | all-gather | bytes 1146880 | tf_op jit(solution)/shard_map/all_gather | solution.py:79
  217.8 0.3 convolution_convert_fusion
  218.1 4.5 %fusion.7 = f32[64,1024]{1,0:T(8,128)S(1)} fusion(bf16[64,3584]{1,0:T(8,128)(2,1)S(1)} %convolution_convert_fusion, bf16[1,3584,1024]{2,1,0:T(8,128)(2,1)} %param.20), kind=kOutput, calls=%fused_computation.7 | convolution fusion | flops 469762048 | bytes 8060928 | tf_op jit(solution)/shard_map/dot_general | solution.py:85
  222.6 8.6 %fusion.12 = bf16[1,64,3584]{2,1,0:T(8,128)(2,1)} fusion(bf16[1,1024,3584]{2,1,0:T(8,128)(2,1)} %param.22, bf16[64,3584]{1,0:T(8,128)(2,1)S(1)} %convolution_convert_fusion, bf16[1,3584,1024]{2,1,0:T(8,128)(2,1)} %param.21, f32[64,1024]{1,0:T(8,128)S(1)} %fusion.7), kind=kOutput, calls=%fused_computation.12 | convolution fusion | flops 940146688 | bytes 15859712 | tf_op jit(solution)/shard_map/dot_general | solution.py:88
  231.2 4.2 %copy.53 = bf16[1,64,3584]{1,0,2:T(2,128)(2,1)S(1)} copy(bf16[1,64,3584]{2,1,0:T(8,128)(2,1)} %fusion.12) | data formatting | bytes 917504 | tf_op jit(solution)/shard_map/convert_element_type | solution.py:90
  235.4 0.5 broadcast.36
  236.0 20.6 %reduce = bf16[3584,64]{1,0:T(8,128)(2,1)} reduce(bf16[3584,1,64]{2,1,0:T(2,128)(2,1)S(1)} %bitcast.64, bf16[]{:T(256)} %broadcast.36), dimensions={1}, to_apply=%bitcast.54.reduce_sub_computation | reduce | bytes 917506
  256.6 2.8 reshape.46
  259.4 4.1 %all-to-all-start = ((bf16[4,2,28672]{2,1,0:T(2,128)(2,1)}), bf16[4,2,28672]{2,1,0:T(2,128)(2,1)}, u32[]{:S(2)}, u32[]{:S(2)}) async-start(bf16[4,2,28672]{2,1,0:T(2,128)(2,1)} %reshape.46), calls=%async_computation.1 | async-start | bytes 917504 | tf_op jit(solution)/shard_map/all_to_all | solution.py:89
  263.6 0.0 all-reduce.6.cloned.1.call-start
  263.6 9.6 %all-to-all-done = bf16[4,2,28672]{2,1,0:T(2,128)(2,1)} async-done(((bf16[4,2,28672]{2,1,0:T(2,128)(2,1)}), bf16[4,2,28672]{2,1,0:T(2,128)(2,1)}, u32[]{:S(2)}, u32[]{:S(2)}) %all-to-all-start) | async-done | bytes 458784 | tf_op jit(solution)/shard_map/all_to_all | solution.py:89
  273.2 2.4 reshape.47
  275.6 1.0 copy.58
  276.7 1.5 copy.55
  278.2 1.1 fusion.24
  279.3 0.0 all-reduce.6.cloned.1.call-update
  279.3 0.0 all-reduce.8.cloned.1.call-start
  279.4 16.4 %all-reduce.6.cloned.1.call-done = bf16[128,896]{1,0:T(8,128)(2,1)} async-done(((bf16[128,896]{1,0:T(8,128)(2,1)}), bf16[128,896]{1,0:T(8,128)(2,1)}) %all-reduce.6.cloned.1.call-update) | async-done | bytes 229392 | tf_op jit(solution)/shard_map/psum | solution.py:94
  295.7 0.0 all-reduce.8.cloned.1.call-update
  295.8 26.2 %all-reduce.8.cloned.1.call-done = bf16[128,896]{1,0:T(8,128)(2,1)} async-done(((bf16[128,896]{1,0:T(8,128)(2,1)}), bf16[128,896]{1,0:T(8,128)(2,1)}) %all-reduce.8.cloned.1.call-update) | async-done | bytes 229392 | tf_op jit(solution)/shard_map/psum | solution.py:94
  322.0 1.9 add_convert_fusion
  (18 shorter events, 0.2 us)
Async XLA Ops:
  6.5 1.3 copy-start
  6.5 97.4 %all-gather.2.cloned.1.call-start = ((), (), s32[]{:S(2)}) async-start(), calls=%async_computation.2 | async-start | bytes 5242880 | tf_op jit(solution)/shard_map/all_gather | solution.py:47
  13.3 90.6 %copy-start.2 = (bf16[32,512,32]{1,2,0:T(8,128)(2,1)S(1)}, bf16[32,512,32]{1,2,0:T(8,128)(2,1)}, u32[]{:S(2)}) copy-start(bf16[32,512,32]{1,2,0:T(8,128)(2,1)} %param.16) | copy-start | bytes 3145732
  20.4 92.7 %copy-start.4 = (s32[128,2]{0,1:T(2,128)S(1)}, s32[128,2]{0,1:T(2,128)}, u32[]{:S(2)}) copy-start(s32[128,2]{0,1:T(2,128)} %param.23) | copy-start | bytes 3076
  20.4 92.7 %copy-start.6 = (s32[8]{0:T(128)S(1)}, s32[8]{0:T(128)}, u32[]{:S(2)}) copy-start(s32[8]{0:T(128)} %param.25) | copy-start | bytes 100
  20.4 165.3 %copy-start.1 = (bf16[128,896]{1,0:T(8,128)(2,1)S(1)}, bf16[128,896]{1,0:T(8,128)(2,1)}, u32[]{:S(2)}) copy-start(bf16[128,896]{1,0:T(8,128)(2,1)} %param.18) | copy-start | bytes 688132
  20.4 178.3 %copy-start.3 = (f32[896]{0:T(1024)S(1)}, f32[896]{0:T(1024)}, u32[]{:S(2)}) copy-start(f32[896]{0:T(1024)} %param.19) | copy-start | bytes 10756
  20.4 130.8 %reduce-scatter.2.cloned.1.call-start = ((), (), s32[]{:S(2)}) async-start(), calls=%async_computation.3 | async-start | bytes 2293760 | tf_op jit(solution)/shard_map/reduce_scatter | solution.py:52
  113.0 72.7 %all-reduce.4.cloned.1.call-start = ((), (), s32[]{:S(2)}) async-start(), calls=%async_computation.4 | async-start | bytes 917504 | tf_op jit(solution)/shard_map/psum | solution.py:53
  231.2 32.4 %copy-start.5 = (f32[128,2]{0,1:T(2,128)S(1)}, f32[128,2]{0,1:T(2,128)}, u32[]{:S(2)}) copy-start(f32[128,2]{0,1:T(2,128)} %param.24) | copy-start | bytes 3076
  259.4 13.8 %all-to-all-start = ((bf16[4,2,28672]{2,1,0:T(2,128)(2,1)}), bf16[4,2,28672]{2,1,0:T(2,128)(2,1)}, u32[]{:S(2)}, u32[]{:S(2)}) async-start(bf16[4,2,28672]{2,1,0:T(2,128)(2,1)} %reshape.46), calls=%async_computation.1 | async-start | bytes 917504 | tf_op jit(solution)/shard_map/all_to_all | solution.py:89
  263.6 32.2 %all-reduce.6.cloned.1.call-start = ((), (), s32[]{:S(2)}) async-start(), calls=%async_computation.5 | async-start | bytes 458752 | tf_op jit(solution)/shard_map/psum | solution.py:94
  279.3 42.6 %all-reduce.8.cloned.1.call-start = ((), (), s32[]{:S(2)}) async-start(), calls=%async_computation.6 | async-start | bytes 458752 | tf_op jit(solution)/shard_map/psum | solution.py:94
Sparse Core Ops, SparseCore 0:
  20.5 83.4 all-gather.1
  113.1 37.9 reduce-scatter.1
  153.5 32.1 all-reduce.3
  279.5 16.2 all-reduce.5
  297.9 24.0 all-reduce.7
